TPU v7x, 32 devices: a whole 2x2x4 slice. The times are simulated.
32 devices in a mesh: cohort: 2 (over y), bx: 16 (over z, x, core).
Axes of the slice: x: 2, y: 2, z: 4, core: 2. Of those that a mesh axis runs over, the one named last changes fastest.
Arguments:
- bold: bfloat16 [256, 12, 4096], P('cohort', None, 'bx'), parts along dimension 0, may hold values from -6 to 6
- nbr_table: int32 [256, 4096], P('cohort', 'bx'), parts along dimension 0, may hold values from -1 to 767, as said below
- subject: int32 [256], P('cohort'), parts along dimension 0, may hold values from 0 to 7
Outputs:
- spread: float32 [8192], P(('cohort', 'bx')), parts along dimension 0
- gram_mean: float32 [256, 128], P('cohort'), parts along dimension 0
There are 2 independent parts, one for each index of `cohort`. A program takes and returns all parts, laid end to end along the dimension named above; each array names one. Nothing has to cross between parts.
Inputs may be any that keep to these rules, and one draw needn't show every extreme that they name: `nbr_table`: rows 125 to 127 are all -1 and row (124) // 2 names the centre itself (256 + its place in its block). Any other entry is -1 or the place, in the window made of the previous block, the centre's own block and the next block (768 voxels in order), of a voxel at most 147 voxels away from the centre in voxel order; no entry names a voxel outside the cohort's 4096 voxels.
All inputs are finite; a program needn't handle non-finite values.
Results may differ from a plain program's by a relative error of at most 0.0003.
Values may be sent and summed in bfloat16 or wider, within the bound.
No kernel may reach another device: no remote copies, remote signals or barrier semaphores. Data moves between devices by JAX's collectives and lax.ppermute only.
A program may use at most 64 MiB of HBM per device.

v0:
```python
import jax
import jax.numpy as jnp
from jax import lax
from jax.sharding import PartitionSpec as P

NB = 125
SUBJ = 8


VARIANCE_FLOOR = 0.05


def extended(cells, sides, width):
    for axis, dim in sides:
        count = lax.axis_size(axis)
        ends = count - 1
        head = lax.slice_in_dim(cells, 0, width, axis=dim)
        tail = lax.slice_in_dim(cells, cells.shape[dim] - width, cells.shape[dim], axis=dim)
        cells = jnp.concatenate(
            [
                lax.ppermute(tail, axis, [(i, (i + 1) % count) for i in range(ends)]),
                cells,
                lax.ppermute(head, axis, [((i + 1) % count, i) for i in range(ends)]),
            ],
            axis=dim,
        )
    return cells


def normalize(series):
    values = series.astype(jnp.float32)
    centred = values - jnp.mean(values, axis=1, keepdims=True)
    divisor = jnp.sqrt(jnp.sum(centred * centred, axis=1, keepdims=True) + 1.0)
    return (centred / divisor).astype(jnp.bfloat16)


def zscore(correl, onehot, counts):
    averages = (
        jnp.einsum("es,ecj->scj", onehot, correl, precision=lax.Precision.HIGHEST)
        / counts[:, None, None]
    )
    expanded = jnp.einsum("es,scj->ecj", onehot, averages, precision=lax.Precision.HIGHEST)
    deviation = correl - expanded
    variance = (
        jnp.einsum("es,ecj->scj", onehot, deviation * deviation, precision=lax.Precision.HIGHEST)
        / counts[:, None, None]
    )
    divisor = jnp.einsum(
        "es,scj->ecj", onehot, jnp.sqrt(variance + VARIANCE_FLOOR), precision=lax.Precision.HIGHEST
    )
    return deviation / divisor


def per_device(bold, nbr_table, subject):
    epochs, points, block_len = bold.shape
    normed = normalize(bold)
    window = extended(normed, (("bx", 2),), block_len)
    window_len = window.shape[2]
    onehot = (subject[:, None] == jnp.arange(SUBJ, dtype=jnp.int32)[None, :]).astype(jnp.float32)
    counts = jnp.maximum(jnp.sum(onehot, axis=0), 1.0)
    group_len = 16
    group_count = block_len // group_len
    places = jnp.arange(window_len, dtype=jnp.int32)

    def one_group(running, group_id):
        first_col = group_id * group_len
        lookup = lax.dynamic_slice_in_dim(nbr_table, first_col, group_len, 1).T
        relative = jnp.where(lookup >= 0, lookup, -1)
        selector = (relative[:, :, None] == places[None, None, :]).astype(jnp.float32)
        centre = lax.dynamic_slice_in_dim(normed, first_col, group_len, 2)
        products = jnp.einsum("etc,etw->ecw", centre, window, preferred_element_type=jnp.float32)
        correl = jnp.einsum("ecw,cjw->ecj", products, selector, precision=lax.Precision.HIGHEST)
        features = zscore(correl, onehot, counts)
        kernel = (
            jnp.einsum("ecj,fcj->cef", features, features, precision=lax.Precision.HIGHEST) / NB
        )
        return (
            running + jnp.sum(kernel, axis=0),
            jnp.sqrt(jnp.sum(kernel * kernel, axis=(1, 2)) / epochs),
        )

    totals, spread = lax.scan(
        one_group,
        jnp.zeros((epochs, epochs), jnp.float32),
        jnp.arange(group_count, dtype=jnp.int32),
    )
    divisor = block_len * lax.axis_size("bx")
    gram_mean = lax.psum(totals, "bx") / divisor
    return (spread.reshape(-1), gram_mean)


def solution(mesh):
    return jax.shard_map(
        per_device,
        mesh=mesh,
        in_specs=(P("cohort", None, "bx"), P("cohort", "bx"), P("cohort")),
        out_specs=(P(("cohort", "bx")), P("cohort", None)),
        check_vma=False,
    )
```

profile of v0, /device:TPU:8, one launch (start us, length us, event | category | flops | bytes accessed | tf_op | source)
XLA Modules:
  0.0 410.3 jit_solution(16473115534681401956)
XLA Ops:
  13.2 4.5 %collective-permute-start.1 = (bf16[128,12,256]{2,0,1:T(8,128)(2,1)S(1)}, bf16[128,12,256]{2,0,1:T(8,128)(2,1)S(1)}, u32[]{:S(2)}, u32[]{:S(2)}) collective-permute-start(bf16[128,12,256]{2,0,1:T(8,128)(2,1)S(1)} %fusion.34), channel_id=1, source_target_pairs={{1,0},{2,1},{3,2},{4,3},{5,4},{6,5},{7,6},{8,7},{9,8},{10,9},{11,1... | collective-permute-start | bytes 2359304 | tf_op jit(solution)/shard_map/ppermute | solution.py:23
  18.0 7.6 %collective-permute-done = bf16[128,12,256]{2,0,1:T(8,128)(2,1)S(1)} collective-permute-done((bf16[128,12,256]{2,0,1:T(8,128)(2,1)S(1)}, bf16[128,12,256]{2,0,1:T(8,128)(2,1)S(1)}, u32[]{:S(2)}, u32[]{:S(2)}) %collective-permute-start) | collective-permute-done | bytes 786464 | tf_op jit(solution)/shard_map/ppermute | solution.py:21
  28.8 277.3 %while.13 = (s32[]{:T(128)}, f32[128,128]{1,0:T(8,128)S(1)}, f32[16,16]{1,0:T(8,128)S(1)}, s32[16]{0:T(128)S(1)}, s32[128,256]{0,1:T(8,128)S(1)}, /*index=5*/bf1...) while((s32[]{:T(128)}, f32[128,128]{1,0:T(8,128)S(1)}, ...), condition=%wide.region_6.7_spmd.clone, body=%wide.region_3.6_spmd.clone.sunk | while | flops 2960470016 | bytes 24029772 | solution.py:82
  32.6 6.0 %fusion.74 = f32[128,16,128]{0,2,1:T(8,128)S(1)} fusion(f32[128,16,768]{2,1,0:T(8,128)S(1)} %fusion.73, s32[16,128]{1,0:T(8,128)S(1)} %compare_select_fusion.2), kind=kOutput, calls=%fused_computation.6.clone.1 | convolution fusion | flops 2417491968 | bytes 7348224 | tf_op jit(solution)/shard_map/while/body/eval_jaxpr/ecw,cjw->ecj/dot_general | solution.py:72
  44.3 1.9 multiply_reduce_fusion.2
  49.9 6.0 %fusion.74 = f32[128,16,128]{0,2,1:T(8,128)S(1)} fusion(f32[128,16,768]{2,1,0:T(8,128)S(1)} %fusion.73, s32[16,128]{1,0:T(8,128)S(1)} %compare_select_fusion.2), kind=kOutput, calls=%fused_computation.6.clone.1 | convolution fusion | flops 2417491968 | bytes 7348224 | tf_op jit(solution)/shard_map/while/body/eval_jaxpr/ecw,cjw->ecj/dot_general | solution.py:72
  61.6 1.9 multiply_reduce_fusion.2
  67.2 6.0 %fusion.74 = f32[128,16,128]{0,2,1:T(8,128)S(1)} fusion(f32[128,16,768]{2,1,0:T(8,128)S(1)} %fusion.73, s32[16,128]{1,0:T(8,128)S(1)} %compare_select_fusion.2), kind=kOutput, calls=%fused_computation.6.clone.1 | convolution fusion | flops 2417491968 | bytes 7348224 | tf_op jit(solution)/shard_map/while/body/eval_jaxpr/ecw,cjw->ecj/dot_general | solution.py:72
  78.9 1.9 multiply_reduce_fusion.2
  84.6 6.0 %fusion.74 = f32[128,16,128]{0,2,1:T(8,128)S(1)} fusion(f32[128,16,768]{2,1,0:T(8,128)S(1)} %fusion.73, s32[16,128]{1,0:T(8,128)S(1)} %compare_select_fusion.2), kind=kOutput, calls=%fused_computation.6.clone.1 | convolution fusion | flops 2417491968 | bytes 7348224 | tf_op jit(solution)/shard_map/while/body/eval_jaxpr/ecw,cjw->ecj/dot_general | solution.py:72
  96.3 1.9 multiply_reduce_fusion.2
  101.9 6.0 %fusion.74 = f32[128,16,128]{0,2,1:T(8,128)S(1)} fusion(f32[128,16,768]{2,1,0:T(8,128)S(1)} %fusion.73, s32[16,128]{1,0:T(8,128)S(1)} %compare_select_fusion.2), kind=kOutput, calls=%fused_computation.6.clone.1 | convolution fusion | flops 2417491968 | bytes 7348224 | tf_op jit(solution)/shard_map/while/body/eval_jaxpr/ecw,cjw->ecj/dot_general | solution.py:72
  113.6 1.9 multiply_reduce_fusion.2
  119.2 6.0 %fusion.74 = f32[128,16,128]{0,2,1:T(8,128)S(1)} fusion(f32[128,16,768]{2,1,0:T(8,128)S(1)} %fusion.73, s32[16,128]{1,0:T(8,128)S(1)} %compare_select_fusion.2), kind=kOutput, calls=%fused_computation.6.clone.1 | convolution fusion | flops 2417491968 | bytes 7348224 | tf_op jit(solution)/shard_map/while/body/eval_jaxpr/ecw,cjw->ecj/dot_general | solution.py:72
  130.9 1.9 multiply_reduce_fusion.2
  136.5 6.0 %fusion.74 = f32[128,16,128]{0,2,1:T(8,128)S(1)} fusion(f32[128,16,768]{2,1,0:T(8,128)S(1)} %fusion.73, s32[16,128]{1,0:T(8,128)S(1)} %compare_select_fusion.2), kind=kOutput, calls=%fused_computation.6.clone.1 | convolution fusion | flops 2417491968 | bytes 7348224 | tf_op jit(solution)/shard_map/while/body/eval_jaxpr/ecw,cjw->ecj/dot_general | solution.py:72
  148.2 1.9 multiply_reduce_fusion.2
  153.8 6.0 %fusion.74 = f32[128,16,128]{0,2,1:T(8,128)S(1)} fusion(f32[128,16,768]{2,1,0:T(8,128)S(1)} %fusion.73, s32[16,128]{1,0:T(8,128)S(1)} %compare_select_fusion.2), kind=kOutput, calls=%fused_computation.6.clone.1 | convolution fusion | flops 2417491968 | bytes 7348224 | tf_op jit(solution)/shard_map/while/body/eval_jaxpr/ecw,cjw->ecj/dot_general | solution.py:72
  165.5 1.9 multiply_reduce_fusion.2
  171.2 6.0 %fusion.74 = f32[128,16,128]{0,2,1:T(8,128)S(1)} fusion(f32[128,16,768]{2,1,0:T(8,128)S(1)} %fusion.73, s32[16,128]{1,0:T(8,128)S(1)} %compare_select_fusion.2), kind=kOutput, calls=%fused_computation.6.clone.1 | convolution fusion | flops 2417491968 | bytes 7348224 | tf_op jit(solution)/shard_map/while/body/eval_jaxpr/ecw,cjw->ecj/dot_general | solution.py:72
  182.9 1.9 multiply_reduce_fusion.2
  188.5 6.0 %fusion.74 = f32[128,16,128]{0,2,1:T(8,128)S(1)} fusion(f32[128,16,768]{2,1,0:T(8,128)S(1)} %fusion.73, s32[16,128]{1,0:T(8,128)S(1)} %compare_select_fusion.2), kind=kOutput, calls=%fused_computation.6.clone.1 | convolution fusion | flops 2417491968 | bytes 7348224 | tf_op jit(solution)/shard_map/while/body/eval_jaxpr/ecw,cjw->ecj/dot_general | solution.py:72
  200.2 1.9 multiply_reduce_fusion.2
  205.8 6.0 %fusion.74 = f32[128,16,128]{0,2,1:T(8,128)S(1)} fusion(f32[128,16,768]{2,1,0:T(8,128)S(1)} %fusion.73, s32[16,128]{1,0:T(8,128)S(1)} %compare_select_fusion.2), kind=kOutput, calls=%fused_computation.6.clone.1 | convolution fusion | flops 2417491968 | bytes 7348224 | tf_op jit(solution)/shard_map/while/body/eval_jaxpr/ecw,cjw->ecj/dot_general | solution.py:72
  217.5 1.9 multiply_reduce_fusion.2
  223.1 6.0 %fusion.74 = f32[128,16,128]{0,2,1:T(8,128)S(1)} fusion(f32[128,16,768]{2,1,0:T(8,128)S(1)} %fusion.73, s32[16,128]{1,0:T(8,128)S(1)} %compare_select_fusion.2), kind=kOutput, calls=%fused_computation.6.clone.1 | convolution fusion | flops 2417491968 | bytes 7348224 | tf_op jit(solution)/shard_map/while/body/eval_jaxpr/ecw,cjw->ecj/dot_general | solution.py:72
  234.8 1.9 multiply_reduce_fusion.2
  240.5 6.0 %fusion.74 = f32[128,16,128]{0,2,1:T(8,128)S(1)} fusion(f32[128,16,768]{2,1,0:T(8,128)S(1)} %fusion.73, s32[16,128]{1,0:T(8,128)S(1)} %compare_select_fusion.2), kind=kOutput, calls=%fused_computation.6.clone.1 | convolution fusion | flops 2417491968 | bytes 7348224 | tf_op jit(solution)/shard_map/while/body/eval_jaxpr/ecw,cjw->ecj/dot_general | solution.py:72
  257.8 6.0 %fusion.74 = f32[128,16,128]{0,2,1:T(8,128)S(1)} fusion(f32[128,16,768]{2,1,0:T(8,128)S(1)} %fusion.73, s32[16,128]{1,0:T(8,128)S(1)} %compare_select_fusion.2), kind=kOutput, calls=%fused_computation.6.clone.1 | convolution fusion | flops 2417491968 | bytes 7348224 | tf_op jit(solution)/shard_map/while/body/eval_jaxpr/ecw,cjw->ecj/dot_general | solution.py:72
  275.1 6.0 %fusion.74 = f32[128,16,128]{0,2,1:T(8,128)S(1)} fusion(f32[128,16,768]{2,1,0:T(8,128)S(1)} %fusion.73, s32[16,128]{1,0:T(8,128)S(1)} %compare_select_fusion.2), kind=kOutput, calls=%fused_computation.6.clone.1 | convolution fusion | flops 2417491968 | bytes 7348224 | tf_op jit(solution)/shard_map/while/body/eval_jaxpr/ecw,cjw->ecj/dot_general | solution.py:72
  292.4 6.0 %fusion.74 = f32[128,16,128]{0,2,1:T(8,128)S(1)} fusion(f32[128,16,768]{2,1,0:T(8,128)S(1)} %fusion.73, s32[16,128]{1,0:T(8,128)S(1)} %compare_select_fusion.2), kind=kOutput, calls=%fused_computation.6.clone.1 | convolution fusion | flops 2417491968 | bytes 7348224 | tf_op jit(solution)/shard_map/while/body/eval_jaxpr/ecw,cjw->ecj/dot_general | solution.py:72
  307.5 94.5 %all-reduce.2.cloned.1.call-done = f32[128,128]{1,0:T(8,128)} async-done(((f32[128,128]{1,0:T(8,128)}), f32[128,128]{1,0:T(8,128)}) %all-reduce.2.cloned.1.call-update) | async-done | bytes 65552 | tf_op jit(solution)/shard_map/psum | solution.py:88
  (207 shorter events, 157.8 us)
Async XLA Ops:
  7.2 10.6 %copy-start.2 = (s32[128,256]{1,0:T(8,128)S(1)}, s32[128,256]{1,0:T(8,128)}, u32[]{:S(2)}) copy-start(s32[128,256]{1,0:T(8,128)} %param.6) | copy-start | bytes 393220
  7.2 10.7 %copy-start.3 = (s32[128]{0:T(128)S(1)}, s32[128]{0:T(128)}, u32[]{:S(2)}) copy-start(s32[128]{0:T(128)} %param.7) | copy-start | bytes 1540
  7.2 394.8 %all-reduce.2.cloned.1.call-start = ((), (), s32[]{:S(2)}) async-start(), calls=%async_computation | async-start | bytes 131072 | tf_op jit(solution)/shard_map/psum | solution.py:88
  11.3 16.0 %copy-start = (bf16[128,12,256]{2,0,1:T(8,128)(2,1)}, bf16[128,12,256]{2,0,1:T(8,128)(2,1)S(1)}, u32[]{:S(2)}) copy-start(bf16[128,12,256]{2,0,1:T(8,128)(2,1)S(1)} %fusion.34) | copy-start | bytes 2359300
  11.3 14.3 %collective-permute-start = (bf16[128,12,256]{2,0,1:T(8,128)(2,1)S(1)}, bf16[128,12,256]{2,0,1:T(8,128)(2,1)S(1)}, u32[]{:S(2)}, u32[]{:S(2)}) collective-permute-start(bf16[128,12,256]{2,0,1:T(8,128)(2,1)S(1)} %fusion.34), channel_id=1, source_target_pairs={{0,1},{1,2},{2,3},{3,4},{4,5},{5,6},{6,7},{7,8},{8,9},{9,10},{10,1... | collective-permute-start | bytes 2359304 | tf_op jit(solution)/shard_map/ppermute | solution.py:21
  13.2 14.1 %collective-permute-start.1 = (bf16[128,12,256]{2,0,1:T(8,128)(2,1)S(1)}, bf16[128,12,256]{2,0,1:T(8,128)(2,1)S(1)}, u32[]{:S(2)}, u32[]{:S(2)}) collective-permute-start(bf16[128,12,256]{2,0,1:T(8,128)(2,1)S(1)} %fusion.34), channel_id=1, source_target_pairs={{1,0},{2,1},{3,2},{4,3},{5,4},{6,5},{7,6},{8,7},{9,8},{10,9},{11,1... | collective-permute-start | bytes 2359304 | tf_op jit(solution)/shard_map/ppermute | solution.py:23
  306.2 0.6 copy-start.1
Sparse Core Ops, SparseCore 0:
  306.9 94.9 all-reduce.1
where the time goes:
time: 411 us; the launch traced here: 410 us
  matrix products  236 us (57%)
  waiting for transfers between devices  104 us (25%)
  local copies, waits for them, and re-layouts  31.5 us (8%)
  between operations  14.2 us (3%)
  loops' own time  11.9 us (3%)
  other arithmetic  6.57 us (2%)
  starting transfers between devices  6.5 us (2%)
    dot_general x16, matrix products, one_group(): jnp.einsum('ecw,cjw->ecj', products, selector, precision=lax.Precision.HI...  96.5 us
    psum x1, waiting for transfers between devices, per_device(): gram_mean = lax.psum(totals, 'bx') / divisor  94.5 us
    dot_general x16, matrix products, one_group(): jnp.einsum('ecj,fcj->cef', features, features, precision=lax.Precision.HI...  31 us
    dot_general x16, matrix products, zscore(): jnp.einsum('es,scj->ecj', onehot, averages, precision=lax.Precision.HIGHEST)  29.2 us
    dot_general x16, matrix products, zscore(): jnp.einsum('es,scj->ecj', onehot, jnp.sqrt(variance + VARIANCE_FLOOR), pr...  29 us
    dynamic_slice x16, local copies, waits for them, and re-layouts, one_group(): centre = lax.dynamic_slice_in_dim(normed, first_col, group_len, 2)  18.8 us
    dot_general x16, matrix products, one_group(): jnp.einsum('etc,etw->ecw', centre, window, preferred_element_type=jnp.flo...  18 us
    dot_general x16, matrix products, zscore(): jnp.einsum('es,ecj->scj', onehot, deviation * deviation, precision=lax.Pr...  16.4 us
  transfers between devices with their start and end apart: 3, of which 3 were waited for; matrix products, arithmetic and copies ran while one was open for 0% of the time, Pallas kernels for 0%

commit v1 on v0

v1 whole, which is shorter than its diff:
```python
import functools

import jax
import jax.numpy as jnp
from jax import lax
from jax.experimental import pallas as pl
from jax.experimental.pallas import tpu as pltpu
from jax.sharding import PartitionSpec as P

NB = 125
VARIANCE_FLOOR = 0.05
REACH = 147
LANES = 128
GROUP = 64
WINDOW = 384
HALO = (WINDOW - GROUP) // 2
TPAD = 16
ECHUNK = 16


def normalize(series):
    values = series.astype(jnp.float32)
    centred = values - jnp.mean(values, axis=1, keepdims=True)
    divisor = jnp.sqrt(jnp.sum(centred * centred, axis=1, keepdims=True) + 1.0)
    return (centred / divisor).astype(jnp.bfloat16)


def body(sub_col, sub_row, nt, idx, win, spread, gram, lhs, prod, sums):
    epochs = sub_col.shape[0]
    depth = ECHUNK * TPAD
    group_id = pl.program_id(0)
    groups = pl.num_programs(0)
    first = pl.multiple_of(group_id * GROUP, GROUP)
    parity = group_id % 2
    lane0 = pl.multiple_of((group_id // 2) * LANES, LANES)

    @pl.when(group_id == 0)
    def _():
        gram[...] = jnp.zeros_like(gram)

    row_e = lax.broadcasted_iota(jnp.int32, (ECHUNK, depth), 0)
    col_e = lax.broadcasted_iota(jnp.int32, (ECHUNK, depth), 1) // TPAD
    diagonal = row_e == col_e

    def chunk(k, carry):
        at = pl.multiple_of(k * depth, depth)
        for c in range(GROUP):
            row = nt[pl.ds(first + c, 1), pl.ds(at, depth)]
            block = jnp.where(diagonal, jnp.broadcast_to(row, (ECHUNK, depth)), 0.0)
            lhs[c * ECHUNK : (c + 1) * ECHUNK, :] = block.astype(jnp.bfloat16)
        out = jnp.dot(
            lhs[...],
            win[parity, pl.ds(at, depth), pl.ds(lane0, WINDOW)],
            preferred_element_type=jnp.float32,
        )
        to = pl.multiple_of(k * ECHUNK, ECHUNK)
        prod[:, pl.ds(to, ECHUNK), :] = out.reshape(GROUP, ECHUNK, WINDOW)
        return carry

    lax.fori_loop(0, epochs // ECHUNK, chunk, 0)

    same = sub_col[...] == sub_row[...]
    same_f = same.astype(jnp.float32)
    counts = jnp.maximum(jnp.sum(same_f, axis=1, keepdims=True), 1.0)
    inverse = jnp.broadcast_to(1.0 / counts, (epochs, LANES))
    same_b = same_f.astype(jnp.bfloat16)
    same_2 = jnp.concatenate([same_b, same_b], axis=1)

    def select(c):
        place = jnp.broadcast_to(idx[pl.ds(first + c, 1), :], (epochs, LANES))
        low = place & (LANES - 1)
        high = place >> 7
        out = jnp.zeros((epochs, LANES), jnp.float32)
        for tile in range(WINDOW // LANES):
            part = prod[c, :, tile * LANES : (tile + 1) * LANES]
            taken = jnp.take_along_axis(part, low, axis=1, mode="promise_in_bounds")
            out = jnp.where(high == tile, taken, out)
        return out

    def pair(p, carry):
        cs = (2 * p, 2 * p + 1)
        x = jnp.concatenate([select(c) for c in cs], axis=1)
        hi = x.astype(jnp.bfloat16)
        lo = (x - hi.astype(jnp.float32)).astype(jnp.bfloat16)
        inv = jnp.concatenate([inverse, inverse], axis=1)
        mean = jnp.dot(same_2, jnp.concatenate([hi, lo], axis=0), preferred_element_type=jnp.float32) * inv
        dev = x - mean
        var = jnp.dot(same_b, (dev * dev).astype(jnp.bfloat16), preferred_element_type=jnp.float32) * inv
        feat = (dev * lax.rsqrt(var + VARIANCE_FLOOR)).astype(jnp.bfloat16)
        total = None
        for i, c in enumerate(cs):
            f = feat[:, i * LANES : (i + 1) * LANES]
            kern = lax.dot_general(f, f, (((1,), (1,)), ((), ())), preferred_element_type=jnp.float32)
            sums[pl.ds(first + c, 1), :] = jnp.sum(kern * kern, axis=0, keepdims=True)
            total = kern if total is None else total + kern
        gram[...] += total
        return carry

    lax.fori_loop(0, GROUP // 2, pair, 0, unroll=2)

    @pl.when(group_id == groups - 1)
    def _():
        ones = jnp.ones((8, epochs), jnp.float32)
        rows = lax.dot_general(
            ones, sums[...], (((1,), (1,)), ((), ())),
            precision=lax.Precision.HIGHEST, preferred_element_type=jnp.float32,
        )
        spread[...] = jnp.sqrt(rows[:1] * (1.0 / (NB * NB)) / epochs)


def per_device(bold, nbr_table, subject):
    epochs, points, block_len = bold.shape
    count = lax.axis_size("bx")
    ends = count - 1
    head = bold[:, :, :HALO]
    tail = bold[:, :, block_len - HALO :]
    before = lax.ppermute(tail, "bx", [(i, i + 1) for i in range(ends)])
    after = lax.ppermute(head, "bx", [(i + 1, i) for i in range(ends)])
    own = normalize(bold)
    padt = ((0, 0), (0, TPAD - points), (0, 0))
    rows = epochs * TPAD
    nt = jnp.pad(own, padt).reshape(rows, block_len).T.astype(jnp.float32)
    ext = jnp.concatenate([normalize(before), own, normalize(after)], axis=2)
    ext = jnp.pad(ext, padt).reshape(rows, block_len + 2 * HALO)
    width = block_len + 2 * HALO - GROUP
    win = jnp.stack([ext[:, :width], ext[:, GROUP:]])
    centre_group = jnp.arange(block_len, dtype=jnp.int32) // GROUP * GROUP
    start = block_len - HALO + centre_group
    idx = jnp.where(nbr_table >= 0, nbr_table - start[None, :], -1).T
    groups = block_len // GROUP
    slots = nbr_table.shape[0]
    whole = lambda *shape: pl.BlockSpec(shape, lambda g: (0,) * len(shape))
    spread, totals = pl.pallas_call(
        body,
        grid=(groups,),
        in_specs=[
            whole(epochs, 1),
            whole(1, epochs),
            whole(block_len, rows),
            whole(block_len, slots),
            whole(2, rows, width),
        ],
        out_specs=[whole(1, block_len), whole(epochs, epochs)],
        out_shape=[
            jax.ShapeDtypeStruct((1, block_len), jnp.float32),
            jax.ShapeDtypeStruct((epochs, epochs), jnp.float32),
        ],
        scratch_shapes=[
            pltpu.VMEM((GROUP * ECHUNK, ECHUNK * TPAD), jnp.bfloat16),
            pltpu.VMEM((GROUP, epochs, WINDOW), jnp.float32),
            pltpu.VMEM((block_len, epochs), jnp.float32),
        ],
        compiler_params=pltpu.CompilerParams(
            dimension_semantics=("arbitrary",), vmem_limit_bytes=56 * 1024 * 1024
        ),
        name="searchlight",
    )(subject[:, None], subject[None, :], nt, idx, win)
    gram_mean = lax.psum(totals, "bx") / (NB * block_len * count)
    return (spread.reshape(-1), gram_mean)


def solution(mesh):
    return jax.shard_map(
        per_device,
        mesh=mesh,
        in_specs=(P("cohort", None, "bx"), P("cohort", "bx"), P("cohort")),
        out_specs=(P(("cohort", "bx")), P("cohort", None)),
        check_vma=False,
    )
```

time: 411 us -> 227 us (0.55)
  matrix products: 236 us -> 0 us
  Pallas kernels: 0 us -> 91.3 us
  local copies, waits for them, and re-layouts: 31.5 us -> 12.9 us
  waiting for transfers between devices: 104 us -> 89.1 us
  loops' own time: 11.9 us -> 0 us
  other arithmetic: 6.57 us -> 12.5 us
    dot_general x112 -> x0, matrix products: 236 us -> none  [the longest x16 96.5 us: one_group(): jnp.einsum('ecw,cjw->ecj', products, selector, precision=lax.Precision.HI...]
    pallas_call x0 -> x1, Pallas kernels: none -> 91.3 us  [per_device(): pl.pallas_call(body, grid=(groups,), in_specs=[whole(epochs, 1), whole(1,...]
    dynamic_slice x32 -> x0, local copies, waits for them, and re-layouts: 28.1 us -> none  [the longest x16 18.8 us: one_group(): centre = lax.dynamic_slice_in_dim(normed, first_col, group_len, 2)]
    another operation x1 -> x0, loops' own time: 11.9 us -> none  [per_device(): lax.scan(one_group, jnp.zeros((epochs, epochs), jnp.float32), jnp.arange(...]
    ppermute x2, waiting for transfers between devices: 9.27 us -> 0.01 us  [the longest x1 0.01 us: per_device(): after = lax.ppermute(head, 'bx', [(i + 1, i) for i in range(ends)])]
    psum x1, waiting for transfers between devices: 94.5 us -> 89 us  [per_device(): gram_mean = lax.psum(totals, 'bx') / (NB * block_len * count)]
    ppermute x0 -> x2, local copies, waits for them, and re-layouts: none -> 4.73 us  [the longest x1 2.37 us: per_device(): after = lax.ppermute(head, 'bx', [(i + 1, i) for i in range(ends)])]
  transfers between devices with their start and end apart: 3 -> 3, of which waited for: 3 -> 1; matrix products, arithmetic and copies ran while one was open for 0% -> 5% of each run, Pallas kernels for 0% -> 0%
where the time goes in v1:
time: 227 us; the launch traced here: 226 us
  Pallas kernels  91.3 us (40%)
  waiting for transfers between devices  89.1 us (39%)
  between operations  14.2 us (6%)
  local copies, waits for them, and re-layouts  12.9 us (6%)
  other arithmetic  12.5 us (6%)
  starting transfers between devices  6.48 us (3%)
    pallas_call x1, Pallas kernels, per_device(): pl.pallas_call(body, grid=(groups,), in_specs=[whole(epochs, 1), whole(1,...  91.3 us
    psum x1, waiting for transfers between devices, per_device(): gram_mean = lax.psum(totals, 'bx') / (NB * block_len * count)  89 us
  transfers between devices with their start and end apart: 3, of which 1 were waited for; matrix products, arithmetic and copies ran while one was open for 5% of the time, Pallas kernels for 0%

profile of v1, /device:TPU:8, one launch (start us, length us, event | category | flops | bytes accessed | tf_op | source)
XLA Modules:
  0.0 226.4 jit_solution(498278941656241439)
XLA Ops:
  7.2 0.0 all-reduce.4.cloned.1.call-start
  7.2 1.8 fusion.19
  9.1 1.1 copy.26
  10.1 1.9 collective-permute-start
  12.0 1.0 copy.27
  13.1 4.5 %collective-permute-start.1 = (bf16[128,12,160]{0,2,1:T(8,128)(2,1)}, bf16[128,12,160]{0,2,1:T(8,128)(2,1)}, u32[]{:S(2)}, u32[]{:S(2)}) collective-permute-start(bf16[128,12,160]{0,2,1:T(8,128)(2,1)} %copy.27), channel_id=1, source_target_pairs={{1,0},{2,1},{3,2},{4,3},{5,4},{6,5},{7,6},{8,7},{9,8},{10,9},{11,1... | collective-permute-start | bytes 1474568 | tf_op jit(solution)/shard_map/ppermute | solution.py:118
  17.6 0.8 convert_reduce_fusion.2
  18.4 0.9 fusion.15
  19.4 0.7 fusion.16
  20.1 0.1 pad.8
  20.2 0.2 bitcast_convert_fusion
  20.5 0.0 copy-start.1
  20.5 0.0 copy-start.2
  20.5 2.0 copy.18
  22.5 0.1 copy.19
  22.6 0.7 copy.25.sub_col
  23.4 0.7 select_bitcast_fusion.idx
  24.1 2.4 %copy.22 = bf16[128,12,160]{2,1,0:T(8,128)(2,1)S(1)} copy(bf16[128,12,160]{0,2,1:T(8,128)(2,1)} %collective-permute-done) | data formatting | bytes 983040 | tf_op jit(solution)/shard_map/ppermute | solution.py:117
  26.5 0.5 convert_reduce_fusion.1
  27.0 0.6 fusion.13
  27.7 0.4 fusion.14
  28.2 2.4 %copy.24 = bf16[128,12,160]{2,1,0:T(8,128)(2,1)S(1)} copy(bf16[128,12,160]{0,2,1:T(8,128)(2,1)} %collective-permute-done.1) | data formatting | bytes 983040 | tf_op jit(solution)/shard_map/ppermute | solution.py:118
  30.5 0.5 convert_reduce_fusion
  31.1 0.7 fusion.11
  31.8 0.4 fusion.12
  32.2 2.0 fusion.4
  34.2 1.2 slice_bitcast_fusion.1
  35.5 2.3 %pad_maximum_fusion.win = bf16[2,2048,512]{2,1,0:T(8,128)(2,1)} fusion(bf16[1,2048,512]{2,1,0:T(8,128)(2,1)S(1)} %get-tuple-element.7, bf16[1,2048,512]{2,1,0:T(8,128)(2,1)S(1)} %get-tuple-element.6), kind=kLoop, calls=%fused_computation.4 | loop fusion | flops 2097152 | bytes 8388608 | tf_op jit(solution)/shard_map/stack | solution.py:126
  37.8 91.3 %searchlight.1 = (f32[1,256]{1,0:T(1,128)}, f32[128,128]{1,0:T(8,128)}) custom-call(s32[128,1]{1,0:T(8,128)} %copy.25.sub_col, s32[1,128]{1,0:T(1,128)} %bitcast.16, f32[256,2048]{1,0:T(8,128)} %bitcast.15, s32[256,128]{1,0:T(8,128)} %select_bitcast_fusion.idx, bf16[2,2048,512]{2,1,0:T(8,128)(2,1)} %pad_maximum_fusion.win), custom_call_target="tpu_custom_call" | custom-call | tf_op jit(solution)/shard_map/searchlight/pallas_call | solution.py:133
  129.1 0.0 all-reduce.4.cloned.1.call-update
  129.1 89.0 %all-reduce.4.cloned.1.call-done = f32[128,128]{1,0:T(8,128)} async-done(((f32[128,128]{1,0:T(8,128)}), f32[128,128]{1,0:T(8,128)}) %all-reduce.4.cloned.1.call-update) | async-done | bytes 65552 | tf_op jit(solution)/shard_map/psum | solution.py:158
  218.1 1.5 broadcast_multiply_fusion.3
  (13 shorter events, 0.2 us)
Async XLA Ops:
  7.2 10.5 %copy-start = (bf16[128,12,256]{2,0,1:T(8,128)(2,1)S(1)}, bf16[128,12,256]{2,0,1:T(8,128)(2,1)}, u32[]{:S(2)}) copy-start(bf16[128,12,256]{2,0,1:T(8,128)(2,1)} %param.3) | copy-start | bytes 2359300
  7.2 210.9 %all-reduce.4.cloned.1.call-start = ((), (), s32[]{:S(2)}) async-start(), calls=%async_computation | async-start | bytes 131072 | tf_op jit(solution)/shard_map/psum | solution.py:158
  10.1 14.0 %collective-permute-start = (bf16[128,12,160]{0,2,1:T(8,128)(2,1)}, bf16[128,12,160]{0,2,1:T(8,128)(2,1)}, u32[]{:S(2)}, u32[]{:S(2)}) collective-permute-start(bf16[128,12,160]{0,2,1:T(8,128)(2,1)} %copy.26), channel_id=1, source_target_pairs={{0,1},{1,2},{2,3},{3,4},{4,5},{5,6},{6,7},{7,8},{8,9},{9,10},{10,1... | collective-permute-start | bytes 1474568 | tf_op jit(solution)/shard_map/ppermute | solution.py:117
  13.1 15.1 %collective-permute-start.1 = (bf16[128,12,160]{0,2,1:T(8,128)(2,1)}, bf16[128,12,160]{0,2,1:T(8,128)(2,1)}, u32[]{:S(2)}, u32[]{:S(2)}) collective-permute-start(bf16[128,12,160]{0,2,1:T(8,128)(2,1)} %copy.27), channel_id=1, source_target_pairs={{1,0},{2,1},{3,2},{4,3},{5,4},{6,5},{7,6},{8,7},{9,8},{10,9},{11,1... | collective-permute-start | bytes 1474568 | tf_op jit(solution)/shard_map/ppermute | solution.py:118
  20.5 2.1 copy-start.1
  20.5 2.2 copy-start.2
Sparse Core Ops, SparseCore 0:
  129.2 88.8 all-reduce.3

commit v2 on v1

v2 whole, which is shorter than its diff:
```python
import functools

import jax
import jax.numpy as jnp
from jax import lax
from jax.experimental import pallas as pl
from jax.experimental.pallas import tpu as pltpu
from jax.sharding import PartitionSpec as P

NB = 125
VARIANCE_FLOOR = 0.05
REACH = 147
LANES = 128
GROUP = 64
WINDOW = 384
HALO = (WINDOW - GROUP) // 2
TPAD = 16
ECHUNK = 16


def normalize(series):
    values = series.astype(jnp.float32)
    centred = values - jnp.mean(values, axis=1, keepdims=True)
    divisor = jnp.sqrt(jnp.sum(centred * centred, axis=1, keepdims=True) + 1.0)
    return (centred / divisor).astype(jnp.bfloat16)


def body(sub_col, sub_row, nt, idx, win_even, win_odd, spread, gram, lhs, prod, sums, win, xs, devs, feats):
    epochs = sub_col.shape[0]
    depth = ECHUNK * TPAD
    group_id = pl.program_id(0)
    groups = pl.num_programs(0)
    first = pl.multiple_of(group_id * GROUP, GROUP)
    parity = group_id % 2
    lane0 = pl.multiple_of((group_id // 2) * LANES, LANES)

    @pl.when(group_id == 0)
    def _():
        gram[...] = jnp.zeros_like(gram)

    @pl.when(parity == 0)
    def _():
        win[...] = win_even[:, pl.ds(lane0, WINDOW)]

    @pl.when(parity == 1)
    def _():
        win[...] = win_odd[:, pl.ds(lane0, WINDOW)]

    row_e = lax.broadcasted_iota(jnp.int32, (ECHUNK, depth), 0)
    col_e = lax.broadcasted_iota(jnp.int32, (ECHUNK, depth), 1) // TPAD
    diagonal = row_e == col_e

    def chunk(k, carry):
        at = pl.multiple_of(k * depth, depth)
        for c in range(GROUP):
            row = nt[pl.ds(first + c, 1), pl.ds(at, depth)]
            block = jnp.where(diagonal, jnp.broadcast_to(row, (ECHUNK, depth)), 0.0)
            lhs[c * ECHUNK : (c + 1) * ECHUNK, :] = block.astype(jnp.bfloat16)
        out = jnp.dot(lhs[...], win[pl.ds(at, depth), :], preferred_element_type=jnp.float32)
        to = pl.multiple_of(k * ECHUNK, ECHUNK)
        prod[:, pl.ds(to, ECHUNK), :] = out.reshape(GROUP, ECHUNK, WINDOW)
        return carry

    lax.fori_loop(0, epochs // ECHUNK, chunk, 0)

    same = sub_col[...] == sub_row[...]
    same_f = same.astype(jnp.float32)
    counts = jnp.maximum(jnp.sum(same_f, axis=1, keepdims=True), 1.0)
    inverse = jnp.broadcast_to(1.0 / counts, (epochs, 2 * LANES))
    same_b = same_f.astype(jnp.bfloat16)
    same_2 = jnp.concatenate([same_b, same_b], axis=1)

    def select(c):
        place = jnp.broadcast_to(idx[pl.ds(first + c, 1), :], (epochs, LANES))
        low = place & (LANES - 1)
        high = place >> 7
        out = jnp.zeros((epochs, LANES), jnp.float32)
        for tile in range(WINDOW // LANES):
            part = prod[c, :, tile * LANES : (tile + 1) * LANES]
            taken = jnp.take_along_axis(part, low, axis=1, mode="promise_in_bounds")
            out = jnp.where(high == tile, taken, out)
        return out

    xs[...] = jnp.zeros_like(xs)
    devs[...] = jnp.zeros_like(devs)
    feats[...] = jnp.zeros_like(feats)
    pairs = GROUP // 2

    def step(p, carry):
        done = first + 2 * jnp.maximum(p - 3, 0)
        total = None
        for i in range(2):
            f = feats[:, i * LANES : (i + 1) * LANES]
            kern = lax.dot_general(f, f, (((1,), (1,)), ((), ())), preferred_element_type=jnp.float32)
            sums[pl.ds(done + i, 1), :] = jnp.sum(kern * kern, axis=0, keepdims=True)
            total = kern if total is None else total + kern
        dev = devs[...]
        var = jnp.dot(same_b, (dev * dev).astype(jnp.bfloat16), preferred_element_type=jnp.float32) * inverse
        x = xs[...]
        hi = x.astype(jnp.bfloat16)
        lo = (x - hi.astype(jnp.float32)).astype(jnp.bfloat16)
        mean = jnp.dot(same_2, jnp.concatenate([hi, lo], axis=0), preferred_element_type=jnp.float32) * inverse
        gram[...] += total
        feats[...] = (dev * lax.rsqrt(var + VARIANCE_FLOOR)).astype(jnp.bfloat16)
        devs[...] = x - mean
        nxt = 2 * jnp.minimum(p, pairs - 1)
        for i in range(2):
            xs[:, i * LANES : (i + 1) * LANES] = select(nxt + i)
        return carry

    lax.fori_loop(0, pairs + 3, step, 0)

    @pl.when(group_id == groups - 1)
    def _():
        ones = jnp.ones((8, epochs), jnp.float32)
        rows = lax.dot_general(
            ones, sums[...], (((1,), (1,)), ((), ())),
            precision=lax.Precision.HIGHEST, preferred_element_type=jnp.float32,
        )
        spread[...] = jnp.sqrt(rows[:1] * (1.0 / (NB * NB)) / epochs)


def total_over(values, axis):
    count = lax.axis_size(axis)
    if count & (count - 1):
        return lax.psum(values, axis)
    step = 1
    while step < count:
        values = values + lax.ppermute(values, axis, [(i, i ^ step) for i in range(count)])
        step *= 2
    return values


def per_device(bold, nbr_table, subject):
    epochs, points, block_len = bold.shape
    count = lax.axis_size("bx")
    ends = count - 1
    rows = epochs * TPAD
    own = jnp.pad(normalize(bold), ((0, 0), (0, TPAD - points), (0, 0))).reshape(rows, block_len)
    before = lax.ppermute(own[:, block_len - HALO :], "bx", [(i, i + 1) for i in range(ends)])
    after = lax.ppermute(own[:, :HALO], "bx", [(i + 1, i) for i in range(ends)])
    nt = own.T.astype(jnp.float32)
    width = block_len + 2 * HALO - GROUP
    win_even = jnp.concatenate([before, own, after[:, : HALO - GROUP]], axis=1)
    win_odd = jnp.concatenate([before[:, GROUP:], own, after], axis=1)
    centre_group = jnp.arange(block_len, dtype=jnp.int32) // GROUP * GROUP
    start = block_len - HALO + centre_group
    idx = jnp.where(nbr_table >= 0, nbr_table - start[None, :], -1).T
    groups = block_len // GROUP
    slots = nbr_table.shape[0]
    whole = lambda *shape: pl.BlockSpec(shape, lambda g: (0,) * len(shape))
    spread, totals = pl.pallas_call(
        body,
        grid=(groups,),
        in_specs=[
            whole(epochs, 1),
            whole(1, epochs),
            whole(block_len, rows),
            whole(block_len, slots),
            whole(rows, width),
            whole(rows, width),
        ],
        out_specs=[whole(1, block_len), whole(epochs, epochs)],
        out_shape=[
            jax.ShapeDtypeStruct((1, block_len), jnp.float32),
            jax.ShapeDtypeStruct((epochs, epochs), jnp.float32),
        ],
        scratch_shapes=[
            pltpu.VMEM((GROUP * ECHUNK, ECHUNK * TPAD), jnp.bfloat16),
            pltpu.VMEM((GROUP, epochs, WINDOW), jnp.float32),
            pltpu.VMEM((block_len, epochs), jnp.float32),
            pltpu.VMEM((rows, WINDOW), jnp.bfloat16),
            pltpu.VMEM((epochs, 2 * LANES), jnp.float32),
            pltpu.VMEM((epochs, 2 * LANES), jnp.float32),
            pltpu.VMEM((epochs, 2 * LANES), jnp.bfloat16),
        ],
        compiler_params=pltpu.CompilerParams(
            dimension_semantics=("arbitrary",), vmem_limit_bytes=56 * 1024 * 1024
        ),
        name="searchlight",
    )(subject[:, None], subject[None, :], nt, idx, win_even, win_odd)
    gram_mean = total_over(totals, "bx") / (NB * block_len * count)
    return (spread.reshape(-1), gram_mean)


def solution(mesh):
    return jax.shard_map(
        per_device,
        mesh=mesh,
        in_specs=(P("cohort", None, "bx"), P("cohort", "bx"), P("cohort")),
        out_specs=(P(("cohort", "bx")), P("cohort", None)),
        check_vma=False,
    )
```

time: 227 us -> 102 us (0.45)
  waiting for transfers between devices: 89.1 us -> 17 us
  Pallas kernels: 91.3 us -> 50.4 us
  between operations: 14.2 us -> 0.79 us
  starting transfers between devices: 6.48 us -> 12.2 us
  local copies, waits for them, and re-layouts: 12.9 us -> 10.1 us
    psum x1 -> x0, waiting for transfers between devices: 89 us -> none  [per_device(): gram_mean = lax.psum(totals, 'bx') / (NB * block_len * count)]
    pallas_call x1, Pallas kernels: 91.3 us -> 50.4 us  [per_device(): pl.pallas_call(body, grid=(groups,), in_specs=[whole(epochs, 1), whole(1,...]
    ppermute x2 -> x6, waiting for transfers between devices: 0.01 us -> 17 us  [the longest x4 11.7 us: total_over(): lax.ppermute(values, axis, [(i, i ^ step) for i in range(count)])]
    ppermute x2 -> x6, starting transfers between devices: 6.44 us -> 12.2 us  [the longest x4 7.59 us: total_over(): lax.ppermute(values, axis, [(i, i ^ step) for i in range(count)])]
    concatenate x1, other arithmetic: 2.05 us -> 4.88 us  [per_device(): win_odd = jnp.concatenate([before[:, GROUP:], own, after], axis=1)]
    another operation x1 -> x0, other arithmetic: 2.29 us -> none  [per_device(): win = jnp.stack([ext[:, :width], ext[:, GROUP:]])]
  transfers between devices with their start and end apart: 3 -> 6, of which waited for: 1 -> 6; matrix products, arithmetic and copies ran while one was open for 5% -> 7% of each run, Pallas kernels for 0% -> 0%
where the time goes in v2:
time: 102 us; the launch traced here: 101 us
  Pallas kernels  50.4 us (49%)
  waiting for transfers between devices  17 us (17%)
  starting transfers between devices  12.2 us (12%)
  other arithmetic  10.3 us (10%)
  local copies, waits for them, and re-layouts  10.1 us (10%)
    pallas_call x1, Pallas kernels, per_device(): pl.pallas_call(body, grid=(groups,), in_specs=[whole(epochs, 1), whole(1,...  50.4 us
    ppermute x4, waiting for transfers between devices, total_over(): lax.ppermute(values, axis, [(i, i ^ step) for i in range(count)])  11.7 us
    ppermute x4, starting transfers between devices, total_over(): lax.ppermute(values, axis, [(i, i ^ step) for i in range(count)])  7.59 us
    concatenate x1, other arithmetic, per_device(): win_odd = jnp.concatenate([before[:, GROUP:], own, after], axis=1)  4.88 us
    ppermute x1, waiting for transfers between devices, per_device(): lax.ppermute(own[:, block_len - HALO:], 'bx', [(i, i + 1) for i in range(...  3.75 us
    ppermute x1, starting transfers between devices, per_device(): after = lax.ppermute(own[:, :HALO], 'bx', [(i + 1, i) for i in range(ends)])  2.71 us
  transfers between devices with their start and end apart: 6, of which 6 were waited for; matrix products, arithmetic and copies ran while one was open for 7% of the time, Pallas kernels for 0%

profile of v2, /device:TPU:8, one launch (start us, length us, event | category | flops | bytes accessed | tf_op | source)
XLA Modules:
  0.0 100.7 jit_solution(13749056932340791405)
XLA Ops:
  0.6 1.3 %convert_reduce_fusion = f32[128,256]{1,0:T(8,128)S(1)} fusion(bf16[128,12,256]{2,0,1:T(8,128)(2,1)} %param.3), kind=kLoop, calls=%fused_computation.4 | loop fusion | flops 753664 | bytes 917504 | tf_op jit(solution)/shard_map/reduce_sum | solution.py:23
  2.0 1.4 %fusion.2 = f32[128,256]{1,0:T(8,128)S(1)} fusion(bf16[128,12,256]{2,0,1:T(8,128)(2,1)} %param.3, f32[128,256]{1,0:T(8,128)S(1)} %broadcast_multiply_fusion), kind=kLoop, calls=%fused_computation.7 | loop fusion | flops 1540096 | bytes 1048576 | tf_op jit(solution)/shard_map/reduce_sum | solution.py:24
  3.4 0.2 fusion.3
  3.6 0.5 copy.21
  4.1 0.1 pad.4.clone
  4.2 0.5 fusion.6
  4.7 1.2 %copy.14 = bf16[2048,160]{0,1:T(8,128)(2,1)} copy(bf16[2048,160]{1,0:T(8,128)(2,1)S(1)} %get-tuple-element.9) | data formatting | bytes 1310720 | tf_op jit(solution)/shard_map/slice | solution.py:141
  5.9 2.7 %collective-permute-start.1 = (bf16[2048,160]{0,1:T(8,128)(2,1)}, bf16[2048,160]{0,1:T(8,128)(2,1)}, u32[]{:S(2)}, u32[]{:S(2)}) collective-permute-start(bf16[2048,160]{0,1:T(8,128)(2,1)} %copy.14), channel_id=1, source_target_pairs={{1,0},{2,1},{3,2},{4,3},{5,4},{6,5},{7,6},{8,7},{9,8},{10,9},{11,1... | collective-permute-start | bytes 1966088 | tf_op jit(solution)/shard_map/ppermute | solution.py:141
  8.6 1.2 %copy.13 = bf16[2048,160]{0,1:T(8,128)(2,1)} copy(bf16[2048,160]{1,0:T(8,128)(2,1)S(1)} %get-tuple-element.8) | data formatting | bytes 1310720 | tf_op jit(solution)/shard_map/slice | solution.py:140
  9.8 1.9 %collective-permute-start = (bf16[2048,160]{0,1:T(8,128)(2,1)}, bf16[2048,160]{0,1:T(8,128)(2,1)}, u32[]{:S(2)}, u32[]{:S(2)}) collective-permute-start(bf16[2048,160]{0,1:T(8,128)(2,1)} %copy.13), channel_id=1, source_target_pairs={{0,1},{1,2},{2,3},{3,4},{4,5},{5,6},{6,7},{7,8},{8,9},{9,10},{10,1... | collective-permute-start | bytes 1966088 | tf_op jit(solution)/shard_map/ppermute | solution.py:140
  11.8 0.2 convert_bitcast_fusion
  12.0 1.9 %copy.20.nt = f32[256,2048]{1,0:T(8,128)} copy(f32[256,2048]{0,1:T(8,128)S(1)} %convert_bitcast_fusion) | data formatting | bytes 4194304 | tf_op jit(solution)/shard_map/convert_element_type | solution.py:142
  13.9 0.1 copy.11
  14.0 0.7 copy.19.sub_col
  14.8 0.8 select_bitcast_fusion.idx
  15.5 1.5 %collective-permute-done.1 = bf16[2048,160]{0,1:T(8,128)(2,1)} collective-permute-done((bf16[2048,160]{0,1:T(8,128)(2,1)}, bf16[2048,160]{0,1:T(8,128)(2,1)}, u32[]{:S(2)}, u32[]{:S(2)}) %collective-permute-start.1) | collective-permute-done | bytes 655392 | tf_op jit(solution)/shard_map/ppermute | solution.py:141
  17.0 1.4 %copy.15 = bf16[2048,160]{1,0:T(8,128)(2,1)S(1)} copy(bf16[2048,160]{0,1:T(8,128)(2,1)} %collective-permute-done.1) | data formatting | bytes 1310720 | tf_op jit(solution)/shard_map/ppermute | solution.py:141
  18.5 0.9 slice.18
  19.3 3.7 %collective-permute-done = bf16[2048,160]{0,1:T(8,128)(2,1)} collective-permute-done((bf16[2048,160]{0,1:T(8,128)(2,1)}, bf16[2048,160]{0,1:T(8,128)(2,1)}, u32[]{:S(2)}, u32[]{:S(2)}) %collective-permute-start) | collective-permute-done | bytes 655392 | tf_op jit(solution)/shard_map/ppermute | solution.py:140
  23.1 1.4 %copy.16 = bf16[2048,160]{1,0:T(8,128)(2,1)S(1)} copy(bf16[2048,160]{0,1:T(8,128)(2,1)} %collective-permute-done) | data formatting | bytes 1310720 | tf_op jit(solution)/shard_map/ppermute | solution.py:140
  24.5 0.2 slice.19
  24.7 4.9 %pad_maximum_fusion.1 = (bf16[2048,512]{1,0:T(8,128)(2,1)}, bf16[2048,512]{1,0:T(8,128)(2,1)}) fusion(bf16[2048,160]{1,0:T(8,128)(2,1)S(1)} %copy.15, bf16[2048,256]{1,0:T(8,128)(2,1)S(1)} %bitcast.10, bf16[2048,96]{1,0:T(8,128)(2,1)S(1)} %slice.19, bf16[2048,96]{1,0:T(8,128)(2,1)} %slice.18, bf16[2048,160]{1,0:T(8,128)(2,1)S(1)} %copy.16), kind=kLoop, calls=%fused_computation.1 | loop fusion | flops 12582912 | bytes 7340032 | tf_op jit(solution)/shard_map/concatenate | solution.py:145
  29.6 50.4 %searchlight.1 = (f32[1,256]{1,0:T(1,128)}, f32[128,128]{1,0:T(8,128)}) custom-call(s32[128,1]{1,0:T(8,128)} %copy.19.sub_col, s32[1,128]{1,0:T(1,128)} %bitcast.11, f32[256,2048]{1,0:T(8,128)} %copy.20.nt, s32[256,128]{1,0:T(8,128)} %select_bitcast_fusion.idx, bf16[2048,512]{1,0:T(8,128)(2,1)} %get-tuple-element.7.win_even, ...), custom_call_target="tpu_custom_call" | custom-call | tf_op jit(solution)/shard_map/searchlight/pallas_call | solution.py:152
  79.9 4.2 %collective-permute-start.2 = (f32[128,128]{1,0:T(8,128)}, f32[128,128]{1,0:T(8,128)S(1)}, u32[]{:S(2)}, u32[]{:S(2)}) collective-permute-start(f32[128,128]{1,0:T(8,128)} %get-tuple-element.5), channel_id=1, source_target_pairs={{0,1},{1,0},{2,3},{3,2},{4,5},{5,4},{6,7},{7,6},{8,9},{9,8},{10,11... | collective-permute-start | bytes 196616 | tf_op jit(solution)/shard_map/ppermute | solution.py:129
  84.1 1.1 %collective-permute-done.2 = f32[128,128]{1,0:T(8,128)S(1)} collective-permute-done((f32[128,128]{1,0:T(8,128)}, f32[128,128]{1,0:T(8,128)S(1)}, u32[]{:S(2)}, u32[]{:S(2)}) %collective-permute-start.2) | collective-permute-done | bytes 65568 | tf_op jit(solution)/shard_map/ppermute | solution.py:129
  85.3 0.9 add.44
  86.1 0.7 collective-permute-start.3
  86.8 3.7 %collective-permute-done.3 = f32[128,128]{1,0:T(8,128)S(1)} collective-permute-done((f32[128,128]{1,0:T(8,128)S(1)}, f32[128,128]{1,0:T(8,128)S(1)}, u32[]{:S(2)}, u32[]{:S(2)}) %collective-permute-start.3) | collective-permute-done | bytes 65568 | tf_op jit(solution)/shard_map/ppermute | solution.py:129
  90.6 4.3 %collective-permute-done.4 = f32[128,128]{1,0:T(8,128)S(1)} collective-permute-done((f32[128,128]{1,0:T(8,128)S(1)}, f32[128,128]{1,0:T(8,128)S(1)}, u32[]{:S(2)}, u32[]{:S(2)}) %collective-permute-start.4) | collective-permute-done | bytes 65568 | tf_op jit(solution)/shard_map/ppermute | solution.py:129
  94.9 2.6 %collective-permute-start.5 = (f32[128,128]{1,0:T(8,128)S(1)}, f32[128,128]{1,0:T(8,128)S(1)}, u32[]{:S(2)}, u32[]{:S(2)}) collective-permute-start(f32[128,128]{1,0:T(8,128)S(1)} %add.46), channel_id=1, source_target_pairs={{0,8},{1,9},{2,10},{3,11},{4,12},{5,13},{6,14},{7,15},{8,0},{9,1},... | collective-permute-start | bytes 196616 | tf_op jit(solution)/shard_map/ppermute | solution.py:129
  97.5 2.6 %collective-permute-done.5 = f32[128,128]{1,0:T(8,128)S(1)} collective-permute-done((f32[128,128]{1,0:T(8,128)S(1)}, f32[128,128]{1,0:T(8,128)S(1)}, u32[]{:S(2)}, u32[]{:S(2)}) %collective-permute-start.5) | collective-permute-done | bytes 65568 | tf_op jit(solution)/shard_map/ppermute | solution.py:129
  100.1 0.6 add_multiply_fusion
  (12 shorter events, 0.2 us)
Async XLA Ops:
  0.6 2.8 %copy-start = (bf16[128,12,256]{2,0,1:T(8,128)(2,1)S(1)}, bf16[128,12,256]{2,0,1:T(8,128)(2,1)}, u32[]{:S(2)}) copy-start(bf16[128,12,256]{2,0,1:T(8,128)(2,1)} %param.3) | copy-start | bytes 2359300
  5.9 11.2 %collective-permute-start.1 = (bf16[2048,160]{0,1:T(8,128)(2,1)}, bf16[2048,160]{0,1:T(8,128)(2,1)}, u32[]{:S(2)}, u32[]{:S(2)}) collective-permute-start(bf16[2048,160]{0,1:T(8,128)(2,1)} %copy.14), channel_id=1, source_target_pairs={{1,0},{2,1},{3,2},{4,3},{5,4},{6,5},{7,6},{8,7},{9,8},{10,9},{11,1... | collective-permute-start | bytes 1966088 | tf_op jit(solution)/shard_map/ppermute | solution.py:141
  9.8 13.2 %collective-permute-start = (bf16[2048,160]{0,1:T(8,128)(2,1)}, bf16[2048,160]{0,1:T(8,128)(2,1)}, u32[]{:S(2)}, u32[]{:S(2)}) collective-permute-start(bf16[2048,160]{0,1:T(8,128)(2,1)} %copy.13), channel_id=1, source_target_pairs={{0,1},{1,2},{2,3},{3,4},{4,5},{5,6},{6,7},{7,8},{8,9},{9,10},{10,1... | collective-permute-start | bytes 1966088 | tf_op jit(solution)/shard_map/ppermute | solution.py:140
  12.0 1.9 %copy-start.1 = (s32[128,256]{1,0:T(8,128)S(1)}, s32[128,256]{1,0:T(8,128)}, u32[]{:S(2)}) copy-start(s32[128,256]{1,0:T(8,128)} %param.4) | copy-start | bytes 393220
  12.0 2.0 %copy-start.2 = (s32[128]{0:T(128)S(1)}, s32[128]{0:T(128)}, u32[]{:S(2)}) copy-start(s32[128]{0:T(128)} %param.5) | copy-start | bytes 1540
  79.9 5.3 %collective-permute-start.2 = (f32[128,128]{1,0:T(8,128)}, f32[128,128]{1,0:T(8,128)S(1)}, u32[]{:S(2)}, u32[]{:S(2)}) collective-permute-start(f32[128,128]{1,0:T(8,128)} %get-tuple-element.5), channel_id=1, source_target_pairs={{0,1},{1,0},{2,3},{3,2},{4,5},{5,4},{6,7},{7,6},{8,9},{9,8},{10,11... | collective-permute-start | bytes 196616 | tf_op jit(solution)/shard_map/ppermute | solution.py:129
  86.1 4.4 %collective-permute-start.3 = (f32[128,128]{1,0:T(8,128)S(1)}, f32[128,128]{1,0:T(8,128)S(1)}, u32[]{:S(2)}, u32[]{:S(2)}) collective-permute-start(f32[128,128]{1,0:T(8,128)S(1)} %add.44), channel_id=1, source_target_pairs={{0,2},{1,3},{2,0},{3,1},{4,6},{5,7},{6,4},{7,5},{8,10},{9,11},{10,... | collective-permute-start | bytes 196616 | tf_op jit(solution)/shard_map/ppermute | solution.py:129
  90.5 4.3 %collective-permute-start.4 = (f32[128,128]{1,0:T(8,128)S(1)}, f32[128,128]{1,0:T(8,128)S(1)}, u32[]{:S(2)}, u32[]{:S(2)}) collective-permute-start(f32[128,128]{1,0:T(8,128)S(1)} %add.45), channel_id=1, source_target_pairs={{0,4},{1,5},{2,6},{3,7},{4,0},{5,1},{6,2},{7,3},{8,12},{9,13},{10,... | collective-permute-start | bytes 196616 | tf_op jit(solution)/shard_map/ppermute | solution.py:129
  94.9 5.2 %collective-permute-start.5 = (f32[128,128]{1,0:T(8,128)S(1)}, f32[128,128]{1,0:T(8,128)S(1)}, u32[]{:S(2)}, u32[]{:S(2)}) collective-permute-start(f32[128,128]{1,0:T(8,128)S(1)} %add.46), channel_id=1, source_target_pairs={{0,8},{1,9},{2,10},{3,11},{4,12},{5,13},{6,14},{7,15},{8,0},{9,1},... | collective-permute-start | bytes 196616 | tf_op jit(solution)/shard_map/ppermute | solution.py:129

commit v3 on v2

--- a/solution.py
+++ b/solution.py
@@ -16,6 +16,7 @@
 HALO = (WINDOW - GROUP) // 2
 TPAD = 16
 ECHUNK = 16
+BATCH = 8
 
 
 def normalize(series):
@@ -25,26 +26,40 @@
     return (centred / divisor).astype(jnp.bfloat16)
 
 
-def body(sub_col, sub_row, nt, idx, win_even, win_odd, spread, gram, lhs, prod, sums, win, xs, devs, feats):
+def body(sub_col, sub_row, nt, idx, before, own, after, spread, gram, lhs, prod, sums, win, xs, devs, feats):
     epochs = sub_col.shape[0]
     depth = ECHUNK * TPAD
     group_id = pl.program_id(0)
     groups = pl.num_programs(0)
     first = pl.multiple_of(group_id * GROUP, GROUP)
-    parity = group_id % 2
-    lane0 = pl.multiple_of((group_id // 2) * LANES, LANES)
 
     @pl.when(group_id == 0)
     def _():
         gram[...] = jnp.zeros_like(gram)
-
-    @pl.when(parity == 0)
-    def _():
-        win[...] = win_even[:, pl.ds(lane0, WINDOW)]
-
-    @pl.when(parity == 1)
-    def _():
-        win[...] = win_odd[:, pl.ds(lane0, WINDOW)]
+        xs[...] = jnp.zeros_like(xs)
+        devs[...] = jnp.zeros_like(devs)
+        feats[...] = jnp.zeros_like(feats)
+
+    for shift in range(0, own.shape[1], GROUP):
+
+        @pl.when(group_id == shift // GROUP)
+        def _(shift=shift):
+            def fill(r, carry):
+                at = pl.ds(pl.multiple_of(r * depth, depth), depth)
+                parts = []
+                left = HALO - shift
+                if left > 0:
+                    parts.append(before[at, shift:])
+                low = max(-left, 0)
+                high = min(own.shape[1], WINDOW - left)
+                parts.append(own[at, low:high])
+                rest = WINDOW - left - high
+                if rest > 0:
+                    parts.append(after[at, :rest])
+                win[at, :] = jnp.concatenate(parts, axis=1)
+                return carry
+
+            lax.fori_loop(0, own.shape[0] // depth, fill, 0)
 
     row_e = lax.broadcasted_iota(jnp.int32, (ECHUNK, depth), 0)
     col_e = lax.broadcasted_iota(jnp.int32, (ECHUNK, depth), 1) // TPAD
@@ -66,7 +81,7 @@
     same = sub_col[...] == sub_row[...]
     same_f = same.astype(jnp.float32)
     counts = jnp.maximum(jnp.sum(same_f, axis=1, keepdims=True), 1.0)
-    inverse = jnp.broadcast_to(1.0 / counts, (epochs, 2 * LANES))
+    inverse = jnp.broadcast_to(1.0 / counts, (epochs, BATCH * LANES))
     same_b = same_f.astype(jnp.bfloat16)
     same_2 = jnp.concatenate([same_b, same_b], axis=1)
 
@@ -81,15 +96,12 @@
             out = jnp.where(high == tile, taken, out)
         return out
 
-    xs[...] = jnp.zeros_like(xs)
-    devs[...] = jnp.zeros_like(devs)
-    feats[...] = jnp.zeros_like(feats)
-    pairs = GROUP // 2
+    batches = GROUP // BATCH
 
     def step(p, carry):
-        done = first + 2 * jnp.maximum(p - 3, 0)
+        done = BATCH * jnp.maximum(group_id * batches + p - 3, 0)
         total = None
-        for i in range(2):
+        for i in range(BATCH):
             f = feats[:, i * LANES : (i + 1) * LANES]
             kern = lax.dot_general(f, f, (((1,), (1,)), ((), ())), preferred_element_type=jnp.float32)
             sums[pl.ds(done + i, 1), :] = jnp.sum(kern * kern, axis=0, keepdims=True)
@@ -103,12 +115,13 @@
         gram[...] += total
         feats[...] = (dev * lax.rsqrt(var + VARIANCE_FLOOR)).astype(jnp.bfloat16)
         devs[...] = x - mean
-        nxt = 2 * jnp.minimum(p, pairs - 1)
-        for i in range(2):
+        nxt = BATCH * jnp.minimum(p, batches - 1)
+        for i in range(BATCH):
             xs[:, i * LANES : (i + 1) * LANES] = select(nxt + i)
         return carry
 
-    lax.fori_loop(0, pairs + 3, step, 0)
+    drain = jnp.where(group_id == groups - 1, 3, 0)
+    lax.fori_loop(0, batches + drain, step, 0)
 
     @pl.when(group_id == groups - 1)
     def _():
@@ -140,9 +153,6 @@
     before = lax.ppermute(own[:, block_len - HALO :], "bx", [(i, i + 1) for i in range(ends)])
     after = lax.ppermute(own[:, :HALO], "bx", [(i + 1, i) for i in range(ends)])
     nt = own.T.astype(jnp.float32)
-    width = block_len + 2 * HALO - GROUP
-    win_even = jnp.concatenate([before, own, after[:, : HALO - GROUP]], axis=1)
-    win_odd = jnp.concatenate([before[:, GROUP:], own, after], axis=1)
     centre_group = jnp.arange(block_len, dtype=jnp.int32) // GROUP * GROUP
     start = block_len - HALO + centre_group
     idx = jnp.where(nbr_table >= 0, nbr_table - start[None, :], -1).T
@@ -157,8 +167,9 @@
             whole(1, epochs),
             whole(block_len, rows),
             whole(block_len, slots),
-            whole(rows, width),
-            whole(rows, width),
+            whole(rows, HALO),
+            whole(rows, block_len),
+            whole(rows, HALO),
         ],
         out_specs=[whole(1, block_len), whole(epochs, epochs)],
         out_shape=[
@@ -170,15 +181,15 @@
             pltpu.VMEM((GROUP, epochs, WINDOW), jnp.float32),
             pltpu.VMEM((block_len, epochs), jnp.float32),
             pltpu.VMEM((rows, WINDOW), jnp.bfloat16),
-            pltpu.VMEM((epochs, 2 * LANES), jnp.float32),
-            pltpu.VMEM((epochs, 2 * LANES), jnp.float32),
-            pltpu.VMEM((epochs, 2 * LANES), jnp.bfloat16),
+            pltpu.VMEM((epochs, BATCH * LANES), jnp.float32),
+            pltpu.VMEM((epochs, BATCH * LANES), jnp.float32),
+            pltpu.VMEM((epochs, BATCH * LANES), jnp.bfloat16),
         ],
         compiler_params=pltpu.CompilerParams(
             dimension_semantics=("arbitrary",), vmem_limit_bytes=56 * 1024 * 1024
         ),
         name="searchlight",
-    )(subject[:, None], subject[None, :], nt, idx, win_even, win_odd)
+    )(subject[:, None], subject[None, :], nt, idx, before, own, after)
     gram_mean = total_over(totals, "bx") / (NB * block_len * count)
     return (spread.reshape(-1), gram_mean)
 

time: 102 us -> 90.9 us (0.89)
  Pallas kernels: 50.4 us -> 44.3 us
  other arithmetic: 10.3 us -> 4.27 us
  starting transfers between devices: 12.2 us -> 15.4 us
  waiting for transfers between devices: 17 us -> 13.9 us
    pallas_call x1, Pallas kernels: 50.4 us -> 44.3 us  [per_device(): pl.pallas_call(body, grid=(groups,), in_specs=[whole(epochs, 1), whole(1,...]
    concatenate x1 -> x0, other arithmetic: 4.88 us -> none  [per_device(): win_odd = jnp.concatenate([before[:, GROUP:], own, after], axis=1)]
    ppermute x1, waiting for transfers between devices: 3.75 us -> 1.84 us  [per_device(): lax.ppermute(own[:, block_len - HALO:], 'bx', [(i, i + 1) for i in range(...]
    ppermute x1, starting transfers between devices: 2.71 us -> 4.53 us  [per_device(): after = lax.ppermute(own[:, :HALO], 'bx', [(i + 1, i) for i in range(ends)])]
    ppermute x4, starting transfers between devices: 7.59 us -> 9 us  [total_over(): lax.ppermute(values, axis, [(i, i ^ step) for i in range(count)])]
    reduce_sum x1, other arithmetic: 1.35 us -> 0.21 us  [normalize(): divisor = jnp.sqrt(jnp.sum(centred * centred, axis=1, keepdims=True) + 1.0)]
    slice x2 -> x0, local copies, waits for them, and re-layouts: 1.07 us -> none  [the longest x1 0.85 us: per_device(): win_even = jnp.concatenate([before, own, after[:, :HALO - GROUP]], axis=1)]
  transfers between devices with their start and end apart: 6 -> 6, of which waited for: 6 -> 6; matrix products, arithmetic and copies ran while one was open for 7% -> 8% of each run, Pallas kernels for 0% -> 0%
where the time goes in v3:
time: 90.9 us; the launch traced here: 89.2 us
  Pallas kernels  44.3 us (49%)
  starting transfers between devices  15.4 us (17%)
  waiting for transfers between devices  13.9 us (15%)
  local copies, waits for them, and re-layouts  10.6 us (12%)
  other arithmetic  4.27 us (5%)
    pallas_call x1, Pallas kernels, per_device(): pl.pallas_call(body, grid=(groups,), in_specs=[whole(epochs, 1), whole(1,...  44.3 us
    ppermute x4, waiting for transfers between devices, total_over(): lax.ppermute(values, axis, [(i, i ^ step) for i in range(count)])  11.3 us
    ppermute x4, starting transfers between devices, total_over(): lax.ppermute(values, axis, [(i, i ^ step) for i in range(count)])  9 us
    ppermute x1, starting transfers between devices, per_device(): after = lax.ppermute(own[:, :HALO], 'bx', [(i + 1, i) for i in range(ends)])  4.53 us
    ppermute x1, local copies, waits for them, and re-layouts, per_device(): after = lax.ppermute(own[:, :HALO], 'bx', [(i + 1, i) for i in range(ends)])  2.19 us
    ppermute x1, local copies, waits for them, and re-layouts, per_device(): lax.ppermute(own[:, block_len - HALO:], 'bx', [(i, i + 1) for i in range(...  2.19 us
    ppermute x1, starting transfers between devices, per_device(): lax.ppermute(own[:, block_len - HALO:], 'bx', [(i, i + 1) for i in range(...  1.91 us
    convert_element_type x1, local copies, waits for them, and re-layouts, per_device(): nt = own.T.astype(jnp.float32)  1.85 us
  transfers between devices with their start and end apart: 6, of which 6 were waited for; matrix products, arithmetic and copies ran while one was open for 8% of the time, Pallas kernels for 0%

profile of v3, /device:TPU:8, one launch (start us, length us, event | category | flops | bytes accessed | tf_op | source)
XLA Modules:
  0.0 89.2 jit_solution(14056216096232517427)
XLA Ops:
  0.6 1.3 %convert_reduce_fusion = f32[128,256]{1,0:T(8,128)S(1)} fusion(bf16[128,12,256]{2,0,1:T(8,128)(2,1)} %param.3), kind=kLoop, calls=%fused_computation.2 | loop fusion | flops 753664 | bytes 917504 | tf_op jit(solution)/shard_map/reduce_sum | solution.py:24
  2.0 0.0 copy-done.1
  2.0 0.2 fusion.2
  2.3 0.2 fusion.3
  2.5 0.5 copy.19
  2.9 0.1 pad.4.clone
  3.1 0.5 fusion.6
  3.5 0.0 copy-start.2
  3.5 1.2 %copy.13 = bf16[2048,160]{0,1:T(8,128)(2,1)} copy(bf16[2048,160]{1,0:T(8,128)(2,1)S(1)} %get-tuple-element.7) | data formatting | bytes 1310720 | tf_op jit(solution)/shard_map/slice | solution.py:153
  4.8 1.9 %collective-permute-start = (bf16[2048,160]{0,1:T(8,128)(2,1)}, bf16[2048,160]{0,1:T(8,128)(2,1)}, u32[]{:S(2)}, u32[]{:S(2)}) collective-permute-start(bf16[2048,160]{0,1:T(8,128)(2,1)} %copy.13), channel_id=1, source_target_pairs={{0,1},{1,2},{2,3},{3,4},{4,5},{5,6},{6,7},{7,8},{8,9},{9,10},{10,1... | collective-permute-start | bytes 1966088 | tf_op jit(solution)/shard_map/ppermute | solution.py:153
  6.7 1.2 %copy.14 = bf16[2048,160]{0,1:T(8,128)(2,1)} copy(bf16[2048,160]{1,0:T(8,128)(2,1)S(1)} %get-tuple-element.6) | data formatting | bytes 1310720 | tf_op jit(solution)/shard_map/slice | solution.py:154
  7.9 4.5 %collective-permute-start.1 = (bf16[2048,160]{0,1:T(8,128)(2,1)}, bf16[2048,160]{0,1:T(8,128)(2,1)}, u32[]{:S(2)}, u32[]{:S(2)}) collective-permute-start(bf16[2048,160]{0,1:T(8,128)(2,1)} %copy.14), channel_id=1, source_target_pairs={{1,0},{2,1},{3,2},{4,3},{5,4},{6,5},{7,6},{8,7},{9,8},{10,9},{11,1... | collective-permute-start | bytes 1966088 | tf_op jit(solution)/shard_map/ppermute | solution.py:154
  12.4 0.7 copy.15.sub_col
  13.2 0.1 copy.11
  13.3 0.2 convert_bitcast_fusion
  13.5 1.8 %copy.16.nt = f32[256,2048]{1,0:T(8,128)} copy(f32[256,2048]{0,1:T(8,128)S(1)} %convert_bitcast_fusion) | data formatting | bytes 4194304 | tf_op jit(solution)/shard_map/convert_element_type | solution.py:155
  15.4 0.7 select_bitcast_fusion.idx
  16.1 1.8 %collective-permute-done = bf16[2048,160]{0,1:T(8,128)(2,1)} collective-permute-done((bf16[2048,160]{0,1:T(8,128)(2,1)}, bf16[2048,160]{0,1:T(8,128)(2,1)}, u32[]{:S(2)}, u32[]{:S(2)}) %collective-permute-start) | collective-permute-done | bytes 655392 | tf_op jit(solution)/shard_map/ppermute | solution.py:153
  18.0 2.2 %copy.17.before = bf16[2048,160]{1,0:T(8,128)(2,1)} copy(bf16[2048,160]{0,1:T(8,128)(2,1)} %collective-permute-done) | data formatting | bytes 1310720 | tf_op jit(solution)/shard_map/ppermute | solution.py:153
  20.2 0.7 collective-permute-done.1
  20.9 2.2 %copy.18.after = bf16[2048,160]{1,0:T(8,128)(2,1)} copy(bf16[2048,160]{0,1:T(8,128)(2,1)} %collective-permute-done.1) | data formatting | bytes 1310720 | tf_op jit(solution)/shard_map/ppermute | solution.py:154
  23.1 44.3 %searchlight.1 = (f32[1,256]{1,0:T(1,128)}, f32[128,128]{1,0:T(8,128)}) custom-call(s32[128,1]{1,0:T(8,128)} %copy.15.sub_col, s32[1,128]{1,0:T(1,128)} %bitcast.11, f32[256,2048]{1,0:T(8,128)} %copy.16.nt, s32[256,128]{1,0:T(8,128)} %select_bitcast_fusion.idx, bf16[2048,160]{1,0:T(8,128)(2,1)} %copy.17.before, bf16[2048,256]{1,0:T(8,128)(2,1)} %bitcast.10, ...), custom_call_target="tpu_custom_call" | custom-call | tf_op jit(solution)/shard_map/searchlight/pallas_call | solution.py:162
  67.4 4.4 %collective-permute-start.2 = (f32[128,128]{1,0:T(8,128)}, f32[128,128]{1,0:T(8,128)S(1)}, u32[]{:S(2)}, u32[]{:S(2)}) collective-permute-start(f32[128,128]{1,0:T(8,128)} %get-tuple-element.5), channel_id=1, source_target_pairs={{0,1},{1,0},{2,3},{3,2},{4,5},{5,4},{6,7},{7,6},{8,9},{9,8},{10,11... | collective-permute-start | bytes 196616 | tf_op jit(solution)/shard_map/ppermute | solution.py:142
  71.8 1.1 %collective-permute-done.2 = f32[128,128]{1,0:T(8,128)S(1)} collective-permute-done((f32[128,128]{1,0:T(8,128)}, f32[128,128]{1,0:T(8,128)S(1)}, u32[]{:S(2)}, u32[]{:S(2)}) %collective-permute-start.2) | collective-permute-done | bytes 65568 | tf_op jit(solution)/shard_map/ppermute | solution.py:142
  72.9 0.9 add.44
  73.8 2.8 %collective-permute-start.3 = (f32[128,128]{1,0:T(8,128)S(1)}, f32[128,128]{1,0:T(8,128)S(1)}, u32[]{:S(2)}, u32[]{:S(2)}) collective-permute-start(f32[128,128]{1,0:T(8,128)S(1)} %add.44), channel_id=1, source_target_pairs={{0,2},{1,3},{2,0},{3,1},{4,6},{5,7},{6,4},{7,5},{8,10},{9,11},{10,... | collective-permute-start | bytes 196616 | tf_op jit(solution)/shard_map/ppermute | solution.py:142
  76.5 2.4 %collective-permute-done.3 = f32[128,128]{1,0:T(8,128)S(1)} collective-permute-done((f32[128,128]{1,0:T(8,128)S(1)}, f32[128,128]{1,0:T(8,128)S(1)}, u32[]{:S(2)}, u32[]{:S(2)}) %collective-permute-start.3) | collective-permute-done | bytes 65568 | tf_op jit(solution)/shard_map/ppermute | solution.py:142
  79.0 0.5 collective-permute-start.4
  79.5 3.8 %collective-permute-done.4 = f32[128,128]{1,0:T(8,128)S(1)} collective-permute-done((f32[128,128]{1,0:T(8,128)S(1)}, f32[128,128]{1,0:T(8,128)S(1)}, u32[]{:S(2)}, u32[]{:S(2)}) %collective-permute-start.4) | collective-permute-done | bytes 65568 | tf_op jit(solution)/shard_map/ppermute | solution.py:142
  83.3 1.3 %collective-permute-start.5 = (f32[128,128]{1,0:T(8,128)S(1)}, f32[128,128]{1,0:T(8,128)S(1)}, u32[]{:S(2)}, u32[]{:S(2)}) collective-permute-start(f32[128,128]{1,0:T(8,128)S(1)} %add.46), channel_id=1, source_target_pairs={{0,8},{1,9},{2,10},{3,11},{4,12},{5,13},{6,14},{7,15},{8,0},{9,1},... | collective-permute-start | bytes 196616 | tf_op jit(solution)/shard_map/ppermute | solution.py:142
  84.6 4.0 %collective-permute-done.5 = f32[128,128]{1,0:T(8,128)S(1)} collective-permute-done((f32[128,128]{1,0:T(8,128)S(1)}, f32[128,128]{1,0:T(8,128)S(1)}, u32[]{:S(2)}, u32[]{:S(2)}) %collective-permute-start.5) | collective-permute-done | bytes 65568 | tf_op jit(solution)/shard_map/ppermute | solution.py:142
  88.5 0.6 add_multiply_fusion
  (11 shorter events, 0.1 us)
Async XLA Ops:
  0.6 1.4 %copy-start.1 = (bf16[128,12,256]{2,0,1:T(8,128)(2,1)S(1)}, bf16[128,12,256]{2,0,1:T(8,128)(2,1)}, u32[]{:S(2)}) copy-start(bf16[128,12,256]{2,0,1:T(8,128)(2,1)} %param.3) | copy-start | bytes 2359300
  3.0 10.2 %copy-start = (bf16[128,16,256]{2,1,0:T(8,128)(2,1)}, bf16[128,16,256]{2,1,0:T(8,128)(2,1)S(1)}, u32[]{:S(2)}) copy-start(bf16[128,16,256]{2,1,0:T(8,128)(2,1)S(1)} %pad.4.clone) | copy-start | bytes 3145732
  3.5 8.9 %copy-start.3 = (s32[128]{0:T(128)S(1)}, s32[128]{0:T(128)}, u32[]{:S(2)}) copy-start(s32[128]{0:T(128)} %param.5) | copy-start | bytes 1540
  3.5 9.7 %copy-start.2 = (s32[128,256]{1,0:T(8,128)S(1)}, s32[128,256]{1,0:T(8,128)}, u32[]{:S(2)}) copy-start(s32[128,256]{1,0:T(8,128)} %param.4) | copy-start | bytes 393220
  4.8 13.2 %collective-permute-start = (bf16[2048,160]{0,1:T(8,128)(2,1)}, bf16[2048,160]{0,1:T(8,128)(2,1)}, u32[]{:S(2)}, u32[]{:S(2)}) collective-permute-start(bf16[2048,160]{0,1:T(8,128)(2,1)} %copy.13), channel_id=1, source_target_pairs={{0,1},{1,2},{2,3},{3,4},{4,5},{5,6},{6,7},{7,8},{8,9},{9,10},{10,1... | collective-permute-start | bytes 1966088 | tf_op jit(solution)/shard_map/ppermute | solution.py:153
  7.9 13.0 %collective-permute-start.1 = (bf16[2048,160]{0,1:T(8,128)(2,1)}, bf16[2048,160]{0,1:T(8,128)(2,1)}, u32[]{:S(2)}, u32[]{:S(2)}) collective-permute-start(bf16[2048,160]{0,1:T(8,128)(2,1)} %copy.14), channel_id=1, source_target_pairs={{1,0},{2,1},{3,2},{4,3},{5,4},{6,5},{7,6},{8,7},{9,8},{10,9},{11,1... | collective-permute-start | bytes 1966088 | tf_op jit(solution)/shard_map/ppermute | solution.py:154
  67.4 5.5 %collective-permute-start.2 = (f32[128,128]{1,0:T(8,128)}, f32[128,128]{1,0:T(8,128)S(1)}, u32[]{:S(2)}, u32[]{:S(2)}) collective-permute-start(f32[128,128]{1,0:T(8,128)} %get-tuple-element.5), channel_id=1, source_target_pairs={{0,1},{1,0},{2,3},{3,2},{4,5},{5,4},{6,7},{7,6},{8,9},{9,8},{10,11... | collective-permute-start | bytes 196616 | tf_op jit(solution)/shard_map/ppermute | solution.py:142
  73.8 5.2 %collective-permute-start.3 = (f32[128,128]{1,0:T(8,128)S(1)}, f32[128,128]{1,0:T(8,128)S(1)}, u32[]{:S(2)}, u32[]{:S(2)}) collective-permute-start(f32[128,128]{1,0:T(8,128)S(1)} %add.44), channel_id=1, source_target_pairs={{0,2},{1,3},{2,0},{3,1},{4,6},{5,7},{6,4},{7,5},{8,10},{9,11},{10,... | collective-permute-start | bytes 196616 | tf_op jit(solution)/shard_map/ppermute | solution.py:142
  79.0 4.3 %collective-permute-start.4 = (f32[128,128]{1,0:T(8,128)S(1)}, f32[128,128]{1,0:T(8,128)S(1)}, u32[]{:S(2)}, u32[]{:S(2)}) collective-permute-start(f32[128,128]{1,0:T(8,128)S(1)} %add.45), channel_id=1, source_target_pairs={{0,4},{1,5},{2,6},{3,7},{4,0},{5,1},{6,2},{7,3},{8,12},{9,13},{10,... | collective-permute-start | bytes 196616 | tf_op jit(solution)/shard_map/ppermute | solution.py:142
  83.3 5.2 %collective-permute-start.5 = (f32[128,128]{1,0:T(8,128)S(1)}, f32[128,128]{1,0:T(8,128)S(1)}, u32[]{:S(2)}, u32[]{:S(2)}) collective-permute-start(f32[128,128]{1,0:T(8,128)S(1)} %add.46), channel_id=1, source_target_pairs={{0,8},{1,9},{2,10},{3,11},{4,12},{5,13},{6,14},{7,15},{8,0},{9,1},... | collective-permute-start | bytes 196616 | tf_op jit(solution)/shard_map/ppermute | solution.py:142
